TPU v7x, 32 devices: a whole 2x2x4 slice. The times are simulated.
32 devices in a mesh: grp: 2 (over y), bn: 16 (over z, x, core).
Axes of the slice: x: 2, y: 2, z: 4, core: 2. Of those that a mesh axis runs over, the one named last changes fastest.
Arguments:
- images: bfloat16 [32, 19, 19, 384], P(('grp', 'bn')), parts along dimension 0, may hold values from -56 to 56
- expand_weight: bfloat16 [384, 2304], P('bn'), may hold values from -0.3125 to 0.3125
- expand_gain: float32 [2304], replicated, may hold values from 0.5 to 2
- expand_shift: float32 [2304], replicated, may hold values from -3 to 3
- depth_weight: bfloat16 [25, 2304], replicated, may hold values from -1.25 to 1.25
- depth_gain: float32 [2304], replicated, may hold values from 0.5 to 2
- depth_shift: float32 [2304], replicated, may hold values from -3 to 3
- squeeze_weight: bfloat16 [2304, 96], replicated, may hold values from -0.125 to 0.125
- squeeze_bias: float32 [96], replicated, may hold values from -4 to 4
- excite_weight: bfloat16 [96, 2304], replicated, may hold values from -0.625 to 0.625
- excite_bias: float32 [2304], replicated, may hold values from -4 to 4
- project_weight: bfloat16 [2304, 384], P('bn'), may hold values from -0.125 to 0.125
- project_gain: float32 [384], replicated, may hold values from 0.5 to 2
- project_shift: float32 [384], replicated, may hold values from -3 to 3
- group_table: int32 [32], P('grp'), parts along dimension 0, may hold values from 0 to 1, as said below
Outputs:
- block_output: bfloat16 [32, 19, 19, 384], P(('grp', 'bn')), parts along dimension 0
There are 2 independent parts, one for each index of `grp`. A program takes and returns all parts, laid end to end along the dimension named above; an argument that names none is the same for every part. Nothing has to cross between parts.
Inputs may be any that keep to these rules, and one draw needn't show every extreme that they name: `group_table`: each of the 2 statistics groups holds at least 4 images, placed anywhere among the images.
All inputs are finite; a program needn't handle non-finite values.
Results may differ from a plain program's by a relative error of at most 0.0065.
Values may be sent and summed in bfloat16 or wider, within the bound.
A program may use at most 64 MiB of HBM per device.

v0:
```python
import jax
import jax.numpy as jnp
from jax import lax
from jax.sharding import PartitionSpec as P

KERNEL = 5
STAT_GROUPS = 2
epsilon = 0.001


def normalize(values, centre, inverse, gain, shift):
    return (values.astype(jnp.float32) - centre) * inverse * gain + shift


def depthwise(widened, depth_weight, height, breadth):
    spatial = widened.reshape(height, breadth, widened.shape[-1])
    margin = KERNEL // 2
    padded = jnp.pad(spatial, ((margin, margin), (margin, margin), (0, 0)))
    accumulated = jnp.zeros(spatial.shape, jnp.float32)
    for row_shift in range(KERNEL):
        for col_shift in range(KERNEL):
            window = padded[row_shift : row_shift + height, col_shift : col_shift + breadth]
            accumulated = accumulated + window.astype(jnp.float32) * depth_weight[
                row_shift * KERNEL + col_shift
            ].astype(jnp.float32)
    return accumulated.reshape(height * breadth, spatial.shape[-1]).astype(jnp.bfloat16)


def group_moments(values, selector, population):
    totals = jnp.sum(values, axis=0, dtype=jnp.float32)
    squares = jnp.sum(jnp.square(values.astype(jnp.float32)), axis=0)
    weighted = selector[:, None, None] * jnp.stack([totals, squares])[None]
    summed = lax.psum(weighted, "bn")
    picked = jnp.sum(selector[:, None, None] * summed, axis=0)
    centre = picked[0] / population
    spread = picked[1] / population - centre * centre
    return (centre, lax.rsqrt(spread + epsilon))


def on_device(
    images,
    expand_weight,
    expand_gain,
    expand_shift,
    depth_weight,
    depth_gain,
    depth_shift,
    squeeze_weight,
    squeeze_bias,
    excite_weight,
    excite_bias,
    project_weight,
    project_gain,
    project_shift,
    group_table,
):
    height, breadth, channels = (images.shape[1], images.shape[2], images.shape[3])
    pixels = height * breadth
    flattened = images.reshape(pixels, channels)
    device_rank = lax.axis_index("bn")
    ranks_all = jnp.arange(group_table.shape[0], dtype=jnp.int32)
    my_group = jnp.sum(jnp.where(ranks_all == device_rank, group_table, 0))
    members = jnp.sum((group_table == my_group).astype(jnp.float32))
    population = members * pixels
    selector = (jnp.arange(STAT_GROUPS, dtype=jnp.int32) == my_group).astype(jnp.float32)
    inputs = flattened
    expanded = jnp.dot(
        inputs,
        lax.all_gather(expand_weight, "bn", axis=0, tiled=True),
        preferred_element_type=jnp.float32,
    ).astype(jnp.bfloat16)
    centre, inverse = group_moments(expanded, selector, population)
    widened = jax.nn.silu(normalize(expanded, centre, inverse, expand_gain, expand_shift)).astype(
        jnp.bfloat16
    )
    filtered = depthwise(widened, depth_weight, height, breadth)
    centre, inverse = group_moments(filtered, selector, population)
    activated = jax.nn.silu(normalize(filtered, centre, inverse, depth_gain, depth_shift)).astype(
        jnp.bfloat16
    )
    pooled = (jnp.sum(activated, axis=0, dtype=jnp.float32) / pixels).astype(jnp.bfloat16)[None, :]
    squeezed = jax.nn.silu(
        jnp.dot(pooled, squeeze_weight, preferred_element_type=jnp.float32) + squeeze_bias
    ).astype(jnp.bfloat16)
    excitation = jax.nn.sigmoid(
        jnp.dot(squeezed, excite_weight, preferred_element_type=jnp.float32) + excite_bias
    )
    gated_input = (activated * excitation).astype(jnp.bfloat16)
    inputs = gated_input
    projected = jnp.dot(
        inputs,
        lax.all_gather(project_weight, "bn", axis=0, tiled=True),
        preferred_element_type=jnp.float32,
    ).astype(jnp.bfloat16)
    centre, inverse = group_moments(projected, selector, population)
    output = flattened.astype(jnp.float32) + normalize(
        projected, centre, inverse, project_gain, project_shift
    )
    return output.astype(jnp.bfloat16).reshape(images.shape)


def solution(mesh):
    return jax.shard_map(
        on_device,
        mesh=mesh,
        in_specs=(
            P(("grp", "bn"), None, None, None),
            P("bn", None),
            P(),
            P(),
            P(),
            P(),
            P(),
            P(),
            P(),
            P(),
            P(),
            P("bn", None),
            P(),
            P(),
            P("grp"),
        ),
        out_specs=P(("grp", "bn"), None, None, None),
        check_vma=False,
    )
```

profile of v0, /device:TPU:0, one launch (start us, length us, event | category | flops | bytes accessed | tf_op | source)
XLA Modules:
  0.0 257.8 jit_solution(15007953222312947867)
XLA Ops:
  6.5 0.0 copy-start
  6.5 0.0 all-gather.3.cloned.1.call-start
  6.5 0.7 all-gather.3.cloned.1.call-update
  7.3 0.0 all-gather.5.cloned.1.call-start
  7.3 0.7 all-gather.5.cloned.1.call-update
  8.0 1.3 fusion.15
  9.3 0.6 compare_convert_fusion.1
  10.0 1.9 fusion.16
  11.9 1.9 convert_reduce_fusion.27
  13.7 1.1 convert_reduce_fusion.26
  14.9 1.1 reshape.239
  16.5 0.0 copy-start.2
  16.5 0.0 copy-start.3
  16.6 36.0 %all-gather.3.cloned.1.call-done = bf16[384,2304]{1,0:T(8,128)(2,1)} async-done(((bf16[24,2304]{1,0:T(8,128)(2,1)}), bf16[384,2304]{1,0:T(8,128)(2,1)}) %all-gather.3.cloned.1.call-update) | async-done | bytes 1769488 | tf_op jit(solution)/shard_map/all_gather | solution.py:69
  52.5 3.7 %convert_reduce_fusion = (f32[2304]{0:T(1024)S(1)}, f32[2304]{0:T(1024)S(1)}, bf16[361,2304]{1,0:T(8,128)(2,1)}) fusion(bf16[361,384]{1,0:T(8,128)(2,1)S(1)} %reshape.239, bf16[384,2304]{1,0:T(8,128)(2,1)} %all-gather.3.cloned.1.call-done), kind=kOutput, calls=%fused_computation.2 | convolution fusion | flops 642933504 | bytes 3728640 | tf_op jit(solution)/shard_map/dot_general | solution.py:67
  56.3 0.1 broadcast_multiply_fusion.1
  56.4 59.8 %psum.21 = f32[2,2,2304]{2,1,0:T(2,128)S(1)} all-reduce(f32[2,2,2304]{2,1,0:T(2,128)S(1)} %broadcast_multiply_fusion.1), channel_id=1, replica_groups=mesh['grp'=2,'bn'=16] {'bn'}, use_global_device_ids=true, to_apply=%region_3.4 | all-reduce | flops 9216 | bytes 73728 | tf_op jit(solution)/shard_map/psum | solution.py:33
  116.2 0.1 multiply_reduce_fusion.3
  116.3 0.1 fusion.26
  116.3 0.0 copy-done.2
  116.4 0.0 copy-done.3
  116.4 2.6 %fusion.9 = bf16[361,2304]{1,0:T(8,128)(2,1)S(1)} fusion(bf16[361,2304]{1,0:T(8,128)(2,1)} %get-tuple-element.43, f32[2304]{0:T(1024)S(1)} %copy-done.2, f32[2304]{0:T(1024)S(1)} %copy-done.3, f32[2304]{0:T(1024)S(1)} %get-tuple-element.39, f32[2304]{0:T(1024)S(1)} %get-tuple-element.38), kind=kLoop, calls=%fused_computation.17 | loop fusion | flops 8317440 | bytes 3363840 | tf_op jit(solution)/shard_map/convert_element_type | solution.py:73
  119.0 2.0 reshape.240
  121.0 32.3 %convert_reduce_fusion.2 = (f32[2304]{0:T(1024)S(1)}, f32[2304]{0:T(1024)S(1)}, bf16[19,19,2304]{2,1,0:T(8,128)(2,1)S(1)}) fusion(f32[2304]{0:T(1024)S(1)} %get-tuple-element.34, f32[2304]{0:T(1024)S(1)} %get-tuple-element.35, f32[2304]{0:T(1024)S(1)} %get-tuple-element.12, f32[2304]{0:T(1024)S(1)} %get-tuple-element.13, f32[2304]{0:T(1024)S(1)} %get-tuple-element.14, ...), kind=kLoop, calls=%fused_computation.20 | loop fusion | flops 65703168 | bytes 3575808 | tf_op jit(solution)/shard_map/reduce_sum | solution.py:30
  153.3 0.0 copy-start.4
  153.3 0.0 copy-start.5
  153.3 0.0 copy-start.1
  153.3 0.0 copy-start.9
  153.4 0.0 copy-start.6
  153.4 2.2 reshape.267
  155.6 0.1 broadcast_multiply_fusion
  155.7 57.9 %psum.22 = f32[2,2,2304]{2,1,0:T(2,128)S(1)} all-reduce(f32[2,2,2304]{2,1,0:T(2,128)S(1)} %broadcast_multiply_fusion), channel_id=1, replica_groups=mesh['grp'=2,'bn'=16] {'bn'}, use_global_device_ids=true, to_apply=%region_8.9 | all-reduce | flops 9216 | bytes 73728 | tf_op jit(solution)/shard_map/psum | solution.py:33
  213.6 0.1 multiply_reduce_fusion.2
  213.7 0.1 fusion.25
  213.7 0.0 copy-done.4
  213.7 0.0 copy-done.5
  213.8 1.6 convert_reduce_fusion.1
  215.3 0.0 copy-done
  215.3 0.0 copy-done.1
  215.4 0.0 copy-done.9
  215.4 0.4 convolution_reduce_fusion
  215.8 0.0 copy-done.6
  215.8 0.0 copy-start.7
  215.8 0.0 copy-start.8
  215.9 0.0 all-gather.5.cloned.1.call-done
  215.9 3.9 %fusion.24 = (f32[384]{0:T(512)S(1)}, f32[384]{0:T(512)S(1)}, f32[361,384]{1,0:T(8,128)S(1)}) fusion(bf16[2304,384]{1,0:T(8,128)(2,1)} %all-gather.5.cloned.1.call-done, f32[2304]{0:T(1024)S(1)} %add_divide_fusion, f32[2304]{0:T(1024)S(1)} %copy-done.4, f32[2304]{0:T(1024)S(1)} %copy-done.5, f32[2304]{0:T(1024)S(1)} %get-tuple-element.37, ...), kind=kOutput, calls=%fused_computation.106 | convolution fusion | flops 649452672 | bytes 5700096 | tf_op jit(solution)/shard_map/dot_general | solution.py:90
  219.8 0.1 broadcast_multiply_fusion.2
  219.9 30.0 %psum.23 = f32[2,2,384]{2,1,0:T(2,128)S(1)} all-reduce(f32[2,2,384]{2,1,0:T(2,128)S(1)} %broadcast_multiply_fusion.2), channel_id=1, replica_groups=mesh['grp'=2,'bn'=16] {'bn'}, use_global_device_ids=true, to_apply=%region_13.14 | all-reduce | flops 1536 | bytes 12288 | tf_op jit(solution)/shard_map/psum | solution.py:33
  249.9 0.1 multiply_reduce_fusion.4
  250.0 0.0 copy-done.7
  250.0 0.0 copy-done.8
  250.0 0.1 add_convert_fusion.1
  250.2 0.8 reshape.241
  (13 shorter events, 0.2 us)
Async XLA Ops:
  6.5 208.8 %copy-start = (bf16[96,2304]{1,0:T(8,128)(2,1)S(1)}, bf16[96,2304]{1,0:T(8,128)(2,1)}, u32[]{:S(2)}) copy-start(bf16[96,2304]{1,0:T(8,128)(2,1)} %param.24) | copy-start | bytes 1327108
  6.5 46.0 %all-gather.3.cloned.1.call-start = ((), (), s32[]{:S(2)}) async-start(), calls=%async_computation | async-start | bytes 1880064 | tf_op jit(solution)/shard_map/all_gather | solution.py:69
  7.3 208.6 %all-gather.5.cloned.1.call-start = ((), (), s32[]{:S(2)}) async-start(), calls=%async_computation.1 | async-start | bytes 1880064 | tf_op jit(solution)/shard_map/all_gather | solution.py:92
  16.5 99.8 %copy-start.2 = (f32[2304]{0:T(1024)S(1)}, f32[2304]{0:T(1024)}, u32[]{:S(2)}) copy-start(f32[2304]{0:T(1024)} %param.18) | copy-start | bytes 27652
  16.5 99.8 %copy-start.3 = (f32[2304]{0:T(1024)S(1)}, f32[2304]{0:T(1024)}, u32[]{:S(2)}) copy-start(f32[2304]{0:T(1024)} %param.17) | copy-start | bytes 27652
  153.3 60.4 %copy-start.4 = (f32[2304]{0:T(1024)S(1)}, f32[2304]{0:T(1024)}, u32[]{:S(2)}) copy-start(f32[2304]{0:T(1024)} %param.21) | copy-start | bytes 27652
  153.3 60.4 %copy-start.5 = (f32[2304]{0:T(1024)S(1)}, f32[2304]{0:T(1024)}, u32[]{:S(2)}) copy-start(f32[2304]{0:T(1024)} %param.20) | copy-start | bytes 27652
  153.3 62.0 %copy-start.1 = (bf16[2304,96]{0,1:T(8,128)(2,1)S(1)}, bf16[2304,96]{0,1:T(8,128)(2,1)}, u32[]{:S(2)}) copy-start(bf16[2304,96]{0,1:T(8,128)(2,1)} %param.22) | copy-start | bytes 1327108
  153.3 62.0 %copy-start.9 = (f32[96]{0:T(128)S(1)}, f32[96]{0:T(128)}, u32[]{:S(2)}) copy-start(f32[96]{0:T(128)} %param.23) | copy-start | bytes 1156
  153.4 62.5 %copy-start.6 = (f32[2304]{0:T(1024)S(1)}, f32[2304]{0:T(1024)}, u32[]{:S(2)}) copy-start(f32[2304]{0:T(1024)} %param.25) | copy-start | bytes 27652
  215.8 34.2 %copy-start.7 = (f32[384]{0:T(512)S(1)}, f32[384]{0:T(512)}, u32[]{:S(2)}) copy-start(f32[384]{0:T(512)} %param.28) | copy-start | bytes 4612
  215.8 34.2 %copy-start.8 = (f32[384]{0:T(512)S(1)}, f32[384]{0:T(512)}, u32[]{:S(2)}) copy-start(f32[384]{0:T(512)} %param.27) | copy-start | bytes 4612
Sparse Core Ops, SparseCore 0:
  9.5 42.9 all-gather.2
  54.7 39.2 all-gather.4
where the time goes:
time: 258 us
  blocking collectives  148 us (57%)
  other arithmetic  44.2 us (17%)
  waiting for transfers between devices  37.4 us (14%)
  between operations  14.3 us (6%)
  matrix products  8.06 us (3%)
  local copies, waits for them, and re-layouts  6.24 us (2%)
    psum x3, blocking collectives, group_moments(): summed = lax.psum(weighted, 'bn')  148 us
    all_gather x1, waiting for transfers between devices, on_device(): lax.all_gather(expand_weight, 'bn', axis=0, tiled=True)  36 us
    reduce_sum x1, other arithmetic, group_moments(): totals = jnp.sum(values, axis=0, dtype=jnp.float32)  32.3 us
  transfers between devices with their start and end apart: 2, of which 1 were waited for; matrix products, arithmetic and copies ran while one was open for 21% of the time, Pallas kernels for 0%

commit v1 on v0

--- a/solution.py
+++ b/solution.py
@@ -30,7 +30,9 @@
     totals = jnp.sum(values, axis=0, dtype=jnp.float32)
     squares = jnp.sum(jnp.square(values.astype(jnp.float32)), axis=0)
     weighted = selector[:, None, None] * jnp.stack([totals, squares])[None]
-    summed = lax.psum(weighted, "bn")
+    summed = weighted
+    for hop in (1, 2, 4, 8):
+        summed = summed + lax.ppermute(summed, "bn", [(dev, dev ^ hop) for dev in range(16)])
     picked = jnp.sum(selector[:, None, None] * summed, axis=0)
     centre = picked[0] / population
     spread = picked[1] / population - centre * centre

time: 258 us -> 150 us (0.58)
  blocking collectives: 148 us -> 0 us
  waiting for transfers between devices: 37.4 us -> 77.2 us
  starting transfers between devices: 0.04 us -> 3.46 us
  other arithmetic: 44.2 us -> 40.9 us
    psum x3 -> x0, blocking collectives: 148 us -> none  [group_moments(): summed = lax.psum(weighted, 'bn')]
    ppermute x0 -> x12, waiting for transfers between devices: none -> 34.3 us  [group_moments(): lax.ppermute(summed, 'bn', [(dev, dev ^ hop) for dev in range(16)])]
    all_gather x1, waiting for transfers between devices: 36 us -> 42.1 us  [on_device(): lax.all_gather(expand_weight, 'bn', axis=0, tiled=True)]
    ppermute x0 -> x12, starting transfers between devices: none -> 3.41 us  [group_moments(): lax.ppermute(summed, 'bn', [(dev, dev ^ hop) for dev in range(16)])]
  transfers between devices with their start and end apart: 2 -> 14, of which waited for: 1 -> 13; matrix products, arithmetic and copies ran while one was open for 21% -> 31% of each run, Pallas kernels for 0% -> 0%
where the time goes in v1:
time: 150 us
  waiting for transfers between devices  77.2 us (51%)
  other arithmetic  40.9 us (27%)
  between operations  14.3 us (10%)
  matrix products  8.03 us (5%)
  local copies, waits for them, and re-layouts  6.43 us (4%)
  starting transfers between devices  3.46 us (2%)
    all_gather x1, waiting for transfers between devices, on_device(): lax.all_gather(expand_weight, 'bn', axis=0, tiled=True)  42.1 us
    ppermute x12, waiting for transfers between devices, group_moments(): lax.ppermute(summed, 'bn', [(dev, dev ^ hop) for dev in range(16)])  34.3 us
    reduce_sum x1, other arithmetic, group_moments(): totals = jnp.sum(values, axis=0, dtype=jnp.float32)  31.5 us
    dot_general x1, matrix products, on_device(): jnp.dot(inputs, lax.all_gather(project_weight, 'bn', axis=0, tiled=True),...  3.9 us
    dot_general x1, matrix products, on_device(): jnp.dot(inputs, lax.all_gather(expand_weight, 'bn', axis=0, tiled=True),...  3.71 us
    ppermute x12, starting transfers between devices, group_moments(): lax.ppermute(summed, 'bn', [(dev, dev ^ hop) for dev in range(16)])  3.41 us
  transfers between devices with their start and end apart: 14, of which 13 were waited for; matrix products, arithmetic and copies ran while one was open for 31% of the time, Pallas kernels for 0%

profile of v1, /device:TPU:0, one launch (start us, length us, event | category | flops | bytes accessed | tf_op | source)
XLA Modules:
  0.0 150.3 jit_solution(4046373924541120378)
XLA Ops:
  6.5 0.7 all-gather.3.cloned.1.call-update
  7.3 0.0 all-gather.5.cloned.1.call-start
  7.3 1.1 reshape.239
  8.4 1.3 fusion.15
  9.7 0.6 compare_convert_fusion.1
  10.3 0.0 copy-start.2
  10.4 0.0 copy-start.11
  10.4 0.0 copy-start.3
  10.4 0.0 copy-start.4
  10.4 42.1 %all-gather.3.cloned.1.call-done = bf16[384,2304]{1,0:T(8,128)(2,1)} async-done(((bf16[24,2304]{1,0:T(8,128)(2,1)}), bf16[384,2304]{1,0:T(8,128)(2,1)}) %all-gather.3.cloned.1.call-update) | async-done | bytes 1769488 | tf_op jit(solution)/shard_map/all_gather | solution.py:71
  52.5 3.7 %convert_reduce_fusion = (f32[2304]{0:T(1024)S(1)}, f32[2304]{0:T(1024)S(1)}, bf16[361,2304]{1,0:T(8,128)(2,1)}) fusion(bf16[361,384]{1,0:T(8,128)(2,1)S(1)} %reshape.239, bf16[384,2304]{1,0:T(8,128)(2,1)} %all-gather.3.cloned.1.call-done), kind=kOutput, calls=%fused_computation.2 | convolution fusion | flops 642933504 | bytes 3728640 | tf_op jit(solution)/shard_map/dot_general | solution.py:69
  56.3 0.1 broadcast_multiply_fusion.1
  56.4 0.3 collective-permute-start
  56.7 0.0 all-gather.5.cloned.1.call-update
  56.7 1.0 collective-permute-done
  57.6 0.1 fusion.25
  57.7 0.6 collective-permute-start.1
  58.4 0.5 convert_reduce_fusion.27
  58.8 2.9 %collective-permute-done.1 = f32[2,2,2304]{2,1,0:T(2,128)S(1)} collective-permute-done((f32[2,2,2304]{2,1,0:T(2,128)S(1)}, f32[2,2,2304]{2,1,0:T(2,128)S(1)}, u32[]{:S(2)}, u32[]{:S(2)}) %collective-permute-start.1) | collective-permute-done | bytes 36896 | tf_op jit(solution)/shard_map/ppermute | solution.py:35
  61.8 0.1 fusion.39
  61.8 0.5 collective-permute-start.2
  62.3 0.2 convert_reduce_fusion.26
  62.5 3.4 %collective-permute-done.2 = f32[2,2,2304]{2,1,0:T(2,128)S(1)} collective-permute-done((f32[2,2,2304]{2,1,0:T(2,128)S(1)}, f32[2,2,2304]{2,1,0:T(2,128)S(1)}, u32[]{:S(2)}, u32[]{:S(2)}) %collective-permute-start.2) | collective-permute-done | bytes 36896 | tf_op jit(solution)/shard_map/ppermute | solution.py:35
  65.9 0.7 collective-permute-start.3
  66.6 1.2 fusion.16
  68.5 3.3 %collective-permute-done.3 = f32[2,2,2304]{2,1,0:T(2,128)S(1)} collective-permute-done((f32[2,2,2304]{2,1,0:T(2,128)S(1)}, f32[2,2,2304]{2,1,0:T(2,128)S(1)}, u32[]{:S(2)}, u32[]{:S(2)}) %collective-permute-start.3) | collective-permute-done | bytes 36896 | tf_op jit(solution)/shard_map/ppermute | solution.py:35
  71.8 0.1 multiply_reduce_fusion.3
  71.9 0.1 fusion.29
  72.0 2.6 %fusion.9 = bf16[361,2304]{1,0:T(8,128)(2,1)S(1)} fusion(bf16[361,2304]{1,0:T(8,128)(2,1)} %get-tuple-element.43, f32[2304]{0:T(1024)S(1)} %copy-done.3, f32[2304]{0:T(1024)S(1)} %copy-done.4, f32[2304]{0:T(1024)S(1)} %get-tuple-element.39, f32[2304]{0:T(1024)S(1)} %get-tuple-element.38), kind=kLoop, calls=%fused_computation.17 | loop fusion | flops 8317440 | bytes 3363840 | tf_op jit(solution)/shard_map/convert_element_type | solution.py:75
  74.6 2.2 %reshape.240 = bf16[19,19,2304]{2,1,0:T(8,128)(2,1)} reshape(bf16[361,2304]{1,0:T(8,128)(2,1)S(1)} %fusion.9) | data formatting | bytes 3326976 | tf_op jit(solution)/shard_map/reshape | solution.py:16
  76.8 31.5 %convert_reduce_fusion.2 = (f32[2304]{0:T(1024)S(1)}, f32[2304]{0:T(1024)S(1)}, bf16[19,19,2304]{2,1,0:T(8,128)(2,1)S(1)}) fusion(f32[2304]{0:T(1024)S(1)} %get-tuple-element.34, f32[2304]{0:T(1024)S(1)} %get-tuple-element.35, f32[2304]{0:T(1024)S(1)} %get-tuple-element.12, f32[2304]{0:T(1024)S(1)} %get-tuple-element.13, f32[2304]{0:T(1024)S(1)} %get-tuple-element.14, ...), kind=kLoop, calls=%fused_computation.20 | loop fusion | flops 65703168 | bytes 3575808 | tf_op jit(solution)/shard_map/reduce_sum | solution.py:30
  108.3 0.1 broadcast_multiply_fusion
  108.4 0.1 collective-permute-start.4
  108.5 1.2 collective-permute-done.4
  109.7 0.1 fusion.26
  109.8 0.3 collective-permute-start.5
  110.1 3.7 %collective-permute-done.5 = f32[2,2,2304]{2,1,0:T(2,128)S(1)} collective-permute-done((f32[2,2,2304]{2,1,0:T(2,128)S(1)}, f32[2,2,2304]{2,1,0:T(2,128)S(1)}, u32[]{:S(2)}, u32[]{:S(2)}) %collective-permute-start.5) | collective-permute-done | bytes 36896 | tf_op jit(solution)/shard_map/ppermute | solution.py:35
  113.8 0.1 fusion.38
  113.9 0.1 collective-permute-start.6
  114.0 3.9 %collective-permute-done.6 = f32[2,2,2304]{2,1,0:T(2,128)S(1)} collective-permute-done((f32[2,2,2304]{2,1,0:T(2,128)S(1)}, f32[2,2,2304]{2,1,0:T(2,128)S(1)}, u32[]{:S(2)}, u32[]{:S(2)}) %collective-permute-start.6) | collective-permute-done | bytes 36896 | tf_op jit(solution)/shard_map/ppermute | solution.py:35
  118.0 0.1 collective-permute-start.7
  118.1 2.2 %reshape.267 = f32[361,2304]{1,0:T(8,128)} reshape(bf16[19,19,2304]{2,1,0:T(8,128)(2,1)S(1)} %get-tuple-element.42) | data formatting | bytes 4990464 | tf_op jit(solution)/shard_map/convert_element_type | solution.py:12
  120.3 2.6 %collective-permute-done.7 = f32[2,2,2304]{2,1,0:T(2,128)S(1)} collective-permute-done((f32[2,2,2304]{2,1,0:T(2,128)S(1)}, f32[2,2,2304]{2,1,0:T(2,128)S(1)}, u32[]{:S(2)}, u32[]{:S(2)}) %collective-permute-start.7) | collective-permute-done | bytes 36896 | tf_op jit(solution)/shard_map/ppermute | solution.py:35
  122.9 0.1 multiply_reduce_fusion.2
  123.0 0.1 fusion.28
  123.1 1.6 %convert_reduce_fusion.1 = f32[2304]{0:T(1024)S(1)} fusion(f32[2304]{0:T(1024)S(1)} %copy-done.5, f32[2304]{0:T(1024)S(1)} %copy-done.6, f32[2304]{0:T(1024)S(1)} %get-tuple-element.37, f32[2304]{0:T(1024)S(1)} %get-tuple-element.36, bf16[19,19,2304]{2,1,0:T(8,128)(2,1)S(1)} %get-tuple-element.42), kind=kLoop, calls=%fused_computation.3 | loop fusion | flops 9978624 | bytes 1709568 | tf_op jit(solution)/shard_map/reduce_sum | solution.py:83
  124.7 0.4 convolution_reduce_fusion
  125.1 0.0 copy-start.9
  125.2 0.0 all-gather.5.cloned.1.call-done
  125.2 3.9 %fusion.27 = (f32[384]{0:T(512)S(1)}, f32[384]{0:T(512)S(1)}, f32[361,384]{1,0:T(8,128)S(1)}) fusion(bf16[2304,384]{1,0:T(8,128)(2,1)} %all-gather.5.cloned.1.call-done, f32[2304]{0:T(1024)S(1)} %add_divide_fusion, f32[2304]{0:T(1024)S(1)} %copy-done.5, f32[2304]{0:T(1024)S(1)} %copy-done.6, f32[2304]{0:T(1024)S(1)} %get-tuple-element.37, ...), kind=kOutput, calls=%fused_computation.109 | convolution fusion | flops 649452672 | bytes 5700096 | tf_op jit(solution)/shard_map/dot_general | solution.py:92
  129.1 0.1 broadcast_multiply_fusion.2
  129.2 0.0 collective-permute-start.8
  129.2 1.2 collective-permute-done.8
  130.4 0.1 fusion.24
  130.5 0.4 collective-permute-start.9
  130.8 3.3 %collective-permute-done.9 = f32[2,2,384]{2,1,0:T(2,128)S(1)} collective-permute-done((f32[2,2,384]{2,1,0:T(2,128)S(1)}, f32[2,2,384]{2,1,0:T(2,128)S(1)}, u32[]{:S(2)}, u32[]{:S(2)}) %collective-permute-start.9) | collective-permute-done | bytes 6176 | tf_op jit(solution)/shard_map/ppermute | solution.py:35
  134.1 0.1 fusion.37
  134.2 0.0 collective-permute-start.10
  134.2 3.6 %collective-permute-done.10 = f32[2,2,384]{2,1,0:T(2,128)S(1)} collective-permute-done((f32[2,2,384]{2,1,0:T(2,128)S(1)}, f32[2,2,384]{2,1,0:T(2,128)S(1)}, u32[]{:S(2)}, u32[]{:S(2)}) %collective-permute-start.10) | collective-permute-done | bytes 6176 | tf_op jit(solution)/shard_map/ppermute | solution.py:35
  137.8 0.3 collective-permute-start.11
  138.1 4.2 %collective-permute-done.11 = f32[2,2,384]{2,1,0:T(2,128)S(1)} collective-permute-done((f32[2,2,384]{2,1,0:T(2,128)S(1)}, f32[2,2,384]{2,1,0:T(2,128)S(1)}, u32[]{:S(2)}, u32[]{:S(2)}) %collective-permute-start.11) | collective-permute-done | bytes 6176 | tf_op jit(solution)/shard_map/ppermute | solution.py:35
  142.3 0.1 multiply_reduce_fusion.4
  142.5 0.1 add_convert_fusion.1
  142.6 0.8 reshape.241
  (36 shorter events, 0.2 us)
Async XLA Ops:
  6.5 118.1 %copy-start = (bf16[96,2304]{1,0:T(8,128)(2,1)S(1)}, bf16[96,2304]{1,0:T(8,128)(2,1)}, u32[]{:S(2)}) copy-start(bf16[96,2304]{1,0:T(8,128)(2,1)} %param.24) | copy-start | bytes 1327108
  6.5 46.0 %all-gather.3.cloned.1.call-start = ((), (), s32[]{:S(2)}) async-start(), calls=%async_computation | async-start | bytes 1880064 | tf_op jit(solution)/shard_map/all_gather | solution.py:71
  7.3 117.9 %all-gather.5.cloned.1.call-start = ((), (), s32[]{:S(2)}) async-start(), calls=%async_computation.1 | async-start | bytes 1880064 | tf_op jit(solution)/shard_map/all_gather | solution.py:94
  10.3 48.0 %copy-start.2 = (bf16[25,2304]{1,0:T(8,128)(2,1)S(1)}, bf16[25,2304]{1,0:T(8,128)(2,1)}, u32[]{:S(2)}) copy-start(bf16[25,2304]{1,0:T(8,128)(2,1)} %param.19) | copy-start | bytes 345604
  10.4 56.3 %copy-start.11 = (s32[16]{0:T(128)S(1)}, s32[16]{0:T(128)}, u32[]{:S(2)}) copy-start(s32[16]{0:T(128)} %param.29) | copy-start | bytes 196
  10.4 61.6 %copy-start.3 = (f32[2304]{0:T(1024)S(1)}, f32[2304]{0:T(1024)}, u32[]{:S(2)}) copy-start(f32[2304]{0:T(1024)} %param.18) | copy-start | bytes 27652
  10.4 61.6 %copy-start.4 = (f32[2304]{0:T(1024)S(1)}, f32[2304]{0:T(1024)}, u32[]{:S(2)}) copy-start(f32[2304]{0:T(1024)} %param.17) | copy-start | bytes 27652
  56.4 1.3 collective-permute-start
  57.7 4.0 %collective-permute-start.1 = (f32[2,2,2304]{2,1,0:T(2,128)S(1)}, f32[2,2,2304]{2,1,0:T(2,128)S(1)}, u32[]{:S(2)}, u32[]{:S(2)}) collective-permute-start(f32[2,2,2304]{2,1,0:T(2,128)S(1)} %fusion.25), channel_id=1, source_target_pairs={{0,2},{1,3},{2,0},{3,1},{4,6},{5,7},{6,4},{7,5},{8,10},{9,11},{10,... | collective-permute-start | bytes 110600 | tf_op jit(solution)/shard_map/ppermute | solution.py:35
  61.8 4.0 %collective-permute-start.2 = (f32[2,2,2304]{2,1,0:T(2,128)S(1)}, f32[2,2,2304]{2,1,0:T(2,128)S(1)}, u32[]{:S(2)}, u32[]{:S(2)}) collective-permute-start(f32[2,2,2304]{2,1,0:T(2,128)S(1)} %fusion.39), channel_id=1, source_target_pairs={{0,4},{1,5},{2,6},{3,7},{4,0},{5,1},{6,2},{7,3},{8,12},{9,13},{10,... | collective-permute-start | bytes 110600 | tf_op jit(solution)/shard_map/ppermute | solution.py:35
  65.9 5.9 %collective-permute-start.3 = (f32[2,2,2304]{2,1,0:T(2,128)S(1)}, f32[2,2,2304]{2,1,0:T(2,128)S(1)}, u32[]{:S(2)}, u32[]{:S(2)}) collective-permute-start(f32[2,2,2304]{2,1,0:T(2,128)S(1)} %add.186), channel_id=1, source_target_pairs={{0,8},{1,9},{2,10},{3,11},{4,12},{5,13},{6,14},{7,15},{8,0},{9,1},... | collective-permute-start | bytes 110600 | tf_op jit(solution)/shard_map/ppermute | solution.py:35
  108.3 14.8 %copy-start.5 = (f32[2304]{0:T(1024)S(1)}, f32[2304]{0:T(1024)}, u32[]{:S(2)}) copy-start(f32[2304]{0:T(1024)} %param.21) | copy-start | bytes 27652
  108.3 14.8 %copy-start.6 = (f32[2304]{0:T(1024)S(1)}, f32[2304]{0:T(1024)}, u32[]{:S(2)}) copy-start(f32[2304]{0:T(1024)} %param.20) | copy-start | bytes 27652
  108.4 1.3 collective-permute-start.4
  109.8 4.0 %collective-permute-start.5 = (f32[2,2,2304]{2,1,0:T(2,128)S(1)}, f32[2,2,2304]{2,1,0:T(2,128)S(1)}, u32[]{:S(2)}, u32[]{:S(2)}) collective-permute-start(f32[2,2,2304]{2,1,0:T(2,128)S(1)} %fusion.26), channel_id=1, source_target_pairs={{0,2},{1,3},{2,0},{3,1},{4,6},{5,7},{6,4},{7,5},{8,10},{9,11},{10,... | collective-permute-start | bytes 110600 | tf_op jit(solution)/shard_map/ppermute | solution.py:35
  113.9 4.0 %collective-permute-start.6 = (f32[2,2,2304]{2,1,0:T(2,128)S(1)}, f32[2,2,2304]{2,1,0:T(2,128)S(1)}, u32[]{:S(2)}, u32[]{:S(2)}) collective-permute-start(f32[2,2,2304]{2,1,0:T(2,128)S(1)} %fusion.38), channel_id=1, source_target_pairs={{0,4},{1,5},{2,6},{3,7},{4,0},{5,1},{6,2},{7,3},{8,12},{9,13},{10,... | collective-permute-start | bytes 110600 | tf_op jit(solution)/shard_map/ppermute | solution.py:35
  118.0 4.9 %collective-permute-start.7 = (f32[2,2,2304]{2,1,0:T(2,128)S(1)}, f32[2,2,2304]{2,1,0:T(2,128)S(1)}, u32[]{:S(2)}, u32[]{:S(2)}) collective-permute-start(f32[2,2,2304]{2,1,0:T(2,128)S(1)} %add.218), channel_id=1, source_target_pairs={{0,8},{1,9},{2,10},{3,11},{4,12},{5,13},{6,14},{7,15},{8,0},{9,1},... | collective-permute-start | bytes 110600 | tf_op jit(solution)/shard_map/ppermute | solution.py:35
  118.1 6.6 %copy-start.1 = (bf16[2304,96]{0,1:T(8,128)(2,1)S(1)}, bf16[2304,96]{0,1:T(8,128)(2,1)}, u32[]{:S(2)}) copy-start(bf16[2304,96]{0,1:T(8,128)(2,1)} %param.22) | copy-start | bytes 1327108
  118.1 6.6 %copy-start.10 = (f32[96]{0:T(128)S(1)}, f32[96]{0:T(128)}, u32[]{:S(2)}) copy-start(f32[96]{0:T(128)} %param.23) | copy-start | bytes 1156
  118.1 7.0 %copy-start.7 = (f32[2304]{0:T(1024)S(1)}, f32[2304]{0:T(1024)}, u32[]{:S(2)}) copy-start(f32[2304]{0:T(1024)} %param.25) | copy-start | bytes 27652
  125.1 17.3 %copy-start.8 = (f32[384]{0:T(512)S(1)}, f32[384]{0:T(512)}, u32[]{:S(2)}) copy-start(f32[384]{0:T(512)} %param.28) | copy-start | bytes 4612
  125.1 17.3 %copy-start.9 = (f32[384]{0:T(512)S(1)}, f32[384]{0:T(512)}, u32[]{:S(2)}) copy-start(f32[384]{0:T(512)} %param.27) | copy-start | bytes 4612
  129.2 1.2 collective-permute-start.8
  130.5 3.6 %collective-permute-start.9 = (f32[2,2,384]{2,1,0:T(2,128)S(1)}, f32[2,2,384]{2,1,0:T(2,128)S(1)}, u32[]{:S(2)}, u32[]{:S(2)}) collective-permute-start(f32[2,2,384]{2,1,0:T(2,128)S(1)} %fusion.24), channel_id=1, source_target_pairs={{0,2},{1,3},{2,0},{3,1},{4,6},{5,7},{6,4},{7,5},{8,10},{9,11},{10,... | collective-permute-start | bytes 18440 | tf_op jit(solution)/shard_map/ppermute | solution.py:35
  134.2 3.6 %collective-permute-start.10 = (f32[2,2,384]{2,1,0:T(2,128)S(1)}, f32[2,2,384]{2,1,0:T(2,128)S(1)}, u32[]{:S(2)}, u32[]{:S(2)}) collective-permute-start(f32[2,2,384]{2,1,0:T(2,128)S(1)} %fusion.37), channel_id=1, source_target_pairs={{0,4},{1,5},{2,6},{3,7},{4,0},{5,1},{6,2},{7,3},{8,12},{9,13},{10,... | collective-permute-start | bytes 18440 | tf_op jit(solution)/shard_map/ppermute | solution.py:35
  137.8 4.5 %collective-permute-start.11 = (f32[2,2,384]{2,1,0:T(2,128)S(1)}, f32[2,2,384]{2,1,0:T(2,128)S(1)}, u32[]{:S(2)}, u32[]{:S(2)}) collective-permute-start(f32[2,2,384]{2,1,0:T(2,128)S(1)} %add.233), channel_id=1, source_target_pairs={{0,8},{1,9},{2,10},{3,11},{4,12},{5,13},{6,14},{7,15},{8,0},{9,1},... | collective-permute-start | bytes 18440 | tf_op jit(solution)/shard_map/ppermute | solution.py:35
Sparse Core Ops, SparseCore 0:
  9.5 42.9 all-gather.2
  56.8 39.1 all-gather.4
